TPU v7x, 256 devices: a whole 4x4x8 slice. The times are simulated.
256 devices in a mesh: lon: 32 (over x_hi, z, core), lat: 8 (over y, x_lo).
Axes of the slice: x: 4 (x_hi: 2, x_lo: 2; x = x_hi * 2 + x_lo), y: 4, z: 8, core: 2. Of those that a mesh axis runs over, the one named last changes fastest.
Arguments:
- tokens: bfloat16 [2, 96, 147456], P(None, 'lat', 'lon'), may hold values from -6 to 6
- cotangent: bfloat16 [2, 48, 147456], P(None, 'lat', 'lon'), may hold values from -6 to 6
- kinds_one: int32 [1, 16], P(None, 'lat'), may hold values from 0 to 7
- kinds_two: int32 [1, 8], P(None, 'lat'), may hold values from 0 to 7
- table_one: float32 [8, 6, 3312], replicated, may hold values from -2 to 260
- table_two: float32 [8, 12, 3312], replicated, may hold values from -2 to 260
- gain_one: float32 [192], replicated, may hold values from 0.1 to 1.9
- gain_merge: float32 [768], replicated, may hold values from 0.1 to 1.9
- gain_two: float32 [384], replicated, may hold values from 0.1 to 1.9
- qkv_one: bfloat16 [192, 576], replicated, may hold values from -0.4375 to 0.4375
- proj_one: bfloat16 [192, 192], replicated, may hold values from -0.4375 to 0.4375
- merge_weight: bfloat16 [768, 384], replicated, may hold values from -0.21875 to 0.21875
- qkv_two: bfloat16 [384, 1152], replicated, may hold values from -0.3125 to 0.3125
- proj_two: bfloat16 [384, 384], replicated, may hold values from -0.3125 to 0.3125
Outputs:
- result: bfloat16 [2, 48, 147456], P(None, 'lat', 'lon')
- d_tokens: bfloat16 [2, 96, 147456], P(None, 'lat', 'lon')
- grad_qkv_one: bfloat16 [192, 576], replicated
- grad_proj_one: bfloat16 [192, 192], replicated
- grad_merge: bfloat16 [768, 384], replicated
- grad_qkv_two: bfloat16 [384, 1152], replicated
- grad_proj_two: bfloat16 [384, 384], replicated
All inputs are finite; a program needn't handle non-finite values.
Results may differ from a plain program's by a relative error of at most 0.025.
Values may be sent and summed in bfloat16 or wider, within the bound.
A program may use at most 128 MiB of HBM per device.

v0:
```python
import jax
import jax.numpy as jnp
import numpy as np
from jax import lax
from jax.sharding import PartitionSpec as P

C1 = 192
HEADS1 = 6
HEADS2 = 12
WIN_Z = 2
WIN_LAT = 6
WIN_LON = 12
LEVELS = 2


norm_epsilon = 1e-05
grad_epsilon = 1e-06
masked_score = -1e30


def as_sent(value):
    return jax.tree.map(lambda a: a.astype(jnp.bfloat16) if a.dtype == jnp.float32 else a, value)


def shifted_2(block, axis, distance):
    devices = range(lax.axis_size(axis))
    route = [((i - distance) % len(devices), i) for i in devices]
    return lax.ppermute(block, axis, route)


def relative_table():
    window_size = WIN_Z * WIN_LAT * WIN_LON
    positions = np.arange(window_size)
    level_at = positions // (WIN_LAT * WIN_LON)
    row_at = positions // WIN_LON % WIN_LAT
    col_at = positions % WIN_LON
    joined = (level_at[:, None] * WIN_Z + level_at[None, :]) * (WIN_LAT * WIN_LAT)
    joined = joined + row_at[:, None] * WIN_LAT + row_at[None, :]
    joined = joined * (2 * WIN_LON - 1) + col_at[:, None] - col_at[None, :] + WIN_LON - 1
    return joined.astype(np.int32)


def layer_norm(values, scaling):
    centre = jnp.mean(values, axis=-1, keepdims=True)
    spread = values - centre
    second = jnp.mean(spread * spread, axis=-1, keepdims=True)
    return spread * lax.rsqrt(second + norm_epsilon) * scaling


def to_windows(lattice):
    level_count, row_count, col_count = lattice.shape[:3]
    trailing = lattice.shape[3:]
    trailing_axes = tuple(range(6, 6 + len(trailing)))
    pieces = lattice.reshape(
        (level_count // WIN_Z, WIN_Z, row_count // WIN_LAT, WIN_LAT, col_count // WIN_LON, WIN_LON)
        + trailing
    )
    pieces = pieces.transpose((0, 2, 4, 1, 3, 5) + trailing_axes)
    return pieces.reshape(
        (
            level_count // WIN_Z,
            row_count // WIN_LAT,
            col_count // WIN_LON,
            WIN_Z * WIN_LAT * WIN_LON,
        )
        + trailing
    )


def from_windows(blocks, level_count, row_count, col_count):
    trailing = blocks.shape[4:]
    trailing_axes = tuple(range(6, 6 + len(trailing)))
    pieces = blocks.reshape(
        (level_count // WIN_Z, row_count // WIN_LAT, col_count // WIN_LON, WIN_Z, WIN_LAT, WIN_LON)
        + trailing
    )
    pieces = pieces.transpose((0, 3, 1, 4, 2, 5) + trailing_axes)
    return pieces.reshape((level_count, row_count, col_count) + trailing)


def region_codes(level_count, row_start, row_count, rows_all):
    level_index = jnp.arange(level_count, dtype=jnp.int32)
    level_part = (level_index >= level_count - WIN_Z).astype(jnp.int32) + (
        level_index >= level_count - WIN_Z // 2
    ).astype(jnp.int32)
    row_index = row_start + jnp.arange(row_count, dtype=jnp.int32)
    row_part = (row_index >= rows_all - WIN_LAT).astype(jnp.int32) + (
        row_index >= rows_all - WIN_LAT // 2
    ).astype(jnp.int32)
    return level_part[:, None] * 3 + row_part[None, :]


def attend(
    shifted,
    kind_ids,
    bias_table,
    scaling,
    w_qkv,
    w_proj,
    head_count,
    row_start,
    rows_all,
    probe_qkv,
    probe_proj,
):
    level_count, row_count, col_count, channel_count = shifted.shape
    head_size = channel_count // head_count
    base_values = shifted.astype(jnp.float32)
    normed = layer_norm(base_values, scaling).astype(jnp.bfloat16)
    flat_rows = normed.reshape(-1, channel_count)
    packed = (jnp.dot(flat_rows, w_qkv, preferred_element_type=jnp.float32) + probe_qkv).astype(
        jnp.bfloat16
    )
    packed = to_windows(packed.reshape(level_count, row_count, col_count, 3, head_count, head_size))
    query_rows = packed[..., 0, :, :]
    key_rows = packed[..., 1, :, :]
    value_rows = packed[..., 2, :, :]
    scores = jnp.einsum(
        "abdqhe,abdkhe->abdhqk", query_rows, key_rows, preferred_element_type=jnp.float32
    ) * head_size ** (-0.5)
    chosen = bias_table[kind_ids]
    full_bias = jnp.take(chosen, relative_table(), axis=3)
    scores = scores + full_bias[:, :, None]
    region_ids = region_codes(level_count, row_start, row_count, rows_all)
    tag_values = jnp.broadcast_to(
        region_ids[:, :, None], (level_count, row_count, col_count)
    ).astype(jnp.float32)
    window_tags = to_windows(tag_values)
    allowed = window_tags[..., :, None] == window_tags[..., None, :]
    scores = jnp.where(allowed[:, :, :, None], scores, masked_score)
    row_top = jnp.max(scores, axis=-1, keepdims=True)
    weights = jnp.exp(scores - row_top)
    attn_weights = (weights / jnp.sum(weights, axis=-1, keepdims=True)).astype(jnp.bfloat16)
    attended = jnp.einsum(
        "abdhqk,abdkhe->abdqhe", attn_weights, value_rows, preferred_element_type=jnp.float32
    ).astype(jnp.bfloat16)
    merged_rows = from_windows(attended, level_count, row_count, col_count).reshape(
        -1, channel_count
    )
    result = (
        base_values.reshape(-1, channel_count)
        + jnp.dot(merged_rows, w_proj, preferred_element_type=jnp.float32)
        + probe_proj
    )
    return (result.astype(jnp.bfloat16).reshape(shifted.shape), (flat_rows, merged_rows))


def merge_tokens(level_one, scaling, w_merge, probe_merge):
    level_count, row_count, col_count, channel_count = level_one.shape
    grouped = level_one.reshape(level_count, row_count // 2, 2, col_count // 2, 2, channel_count)
    grouped = grouped.transpose(0, 1, 3, 2, 4, 5).reshape(
        level_count, row_count // 2, col_count // 2, 4 * channel_count
    )
    normed = layer_norm(grouped.astype(jnp.float32), scaling).astype(jnp.bfloat16)
    flat_rows = normed.reshape(-1, 4 * channel_count)
    merged = (jnp.dot(flat_rows, w_merge, preferred_element_type=jnp.float32) + probe_merge).astype(
        jnp.bfloat16
    )
    return (
        merged.reshape(level_count, row_count // 2, col_count // 2, w_merge.shape[1]),
        flat_rows,
    )


def weight_grad(inputs, cot_rows):
    return lax.dot_general(
        inputs,
        cot_rows.astype(jnp.bfloat16),
        (((0,), (0,)), ((), ())),
        preferred_element_type=jnp.float32,
    )


def normalized(gradient):
    scale_back = lax.rsqrt(jnp.mean(gradient * gradient) + grad_epsilon)
    return (gradient * scale_back).astype(jnp.bfloat16)


def lat_move(band_piece, offset):
    return jax.tree.map(
        lambda part, own: part.astype(own.dtype),
        shifted_2(as_sent(band_piece), "lat", offset),
        band_piece,
    )


def lon_move(band_piece, offset):
    return shifted_2(as_sent(band_piece), "lon", offset).astype(band_piece.dtype)


def roll_ahead(lattice, level_step):
    half_lat = WIN_LAT // 2
    half_lon = WIN_LON // 2
    if level_step != 0:
        lattice = jnp.roll(lattice, -level_step, 0)
    lattice = jnp.concatenate([lattice[:, half_lat:], lat_move(lattice[:, :half_lat], -1)], 1)
    return jnp.concatenate([lattice[:, :, half_lon:], lon_move(lattice[:, :, :half_lon], -1)], 2)


def roll_behind(lattice, level_step):
    half_lat = WIN_LAT // 2
    half_lon = WIN_LON // 2
    lattice = jnp.concatenate([lat_move(lattice[:, -half_lat:], 1), lattice[:, :-half_lat]], 1)
    lattice = jnp.concatenate(
        [lon_move(lattice[:, :, -half_lon:], 1), lattice[:, :, :-half_lon]], 2
    )
    if level_step != 0:
        lattice = jnp.roll(lattice, level_step, 0)
    return lattice


def local_pass(shifted, kind_ids, bias_table, scaling, w_qkv, w_proj, head_count):
    level_count, row_count, col_count, channel_count = shifted.shape
    token_count = level_count * row_count * col_count
    row_start = lax.axis_index("lat") * row_count
    rows_all = lax.axis_size("lat") * row_count

    def local_forward(lattice, probe_qkv, probe_proj):
        return attend(
            lattice,
            kind_ids,
            bias_table,
            scaling,
            w_qkv,
            w_proj,
            head_count,
            row_start,
            rows_all,
            probe_qkv,
            probe_proj,
        )

    return jax.vjp(
        local_forward,
        shifted,
        jnp.zeros((token_count, 3 * channel_count), jnp.float32),
        jnp.zeros((token_count, channel_count), jnp.float32),
        has_aux=True,
    )


def merge_pass(level_one, scaling, w_merge):
    token_count = level_one.shape[0] * (level_one.shape[1] // 2) * (level_one.shape[2] // 2)

    def merge_forward(lattice, probe_merge):
        return merge_tokens(lattice, scaling, w_merge, probe_merge)

    return jax.vjp(
        merge_forward,
        level_one,
        jnp.zeros((token_count, w_merge.shape[1]), jnp.float32),
        has_aux=True,
    )


def shards(
    tokens,
    cotangent,
    kinds_one,
    kinds_two,
    table_one,
    table_two,
    gain_one,
    gain_merge,
    gain_two,
    qkv_one,
    proj_one,
    merge_weight,
    qkv_two,
    proj_two,
):
    row_count = tokens.shape[1]
    col_count = tokens.shape[2] // C1
    level_step = WIN_Z // 2
    lattice = tokens.reshape(LEVELS, row_count, col_count, C1)
    shifted_one = roll_ahead(lattice, level_step)
    block_one, pull_one, saved_one = local_pass(
        shifted_one, kinds_one, table_one, gain_one, qkv_one, proj_one, HEADS1
    )
    moved_one = roll_ahead(block_one, 0)
    shifted_two, pull_merge, merged_norm = merge_pass(moved_one, gain_merge, merge_weight)
    block_two, pull_two, saved_two = local_pass(
        shifted_two, kinds_two, table_two, gain_two, qkv_two, proj_two, HEADS2
    )
    level_two = roll_behind(block_two, level_step)
    d_block_two = roll_ahead(cotangent.reshape(level_two.shape), level_step)
    d_shift_two, d_packed_two, d_out_two = pull_two(d_block_two)
    raw_qkv_two = weight_grad(saved_two[0], d_packed_two)
    raw_proj_two = weight_grad(saved_two[1], d_out_two)
    d_moved_one, d_probe_merge = pull_merge(d_shift_two)
    raw_merge = weight_grad(merged_norm, d_probe_merge)
    d_block_one = roll_behind(d_moved_one, 0)
    d_shift_one, d_packed_one, d_out_one = pull_one(d_block_one)
    raw_qkv_one = weight_grad(saved_one[0], d_packed_one)
    raw_proj_one = weight_grad(saved_one[1], d_out_one)
    d_tokens = roll_behind(d_shift_one, level_step)
    raw_qkv_one, raw_proj_one, raw_merge, raw_qkv_two, raw_proj_two = lax.psum(
        (raw_qkv_one, raw_proj_one, raw_merge, raw_qkv_two, raw_proj_two), ("lon", "lat")
    )
    return (
        level_two.reshape(LEVELS, level_two.shape[1], -1),
        d_tokens.reshape(LEVELS, row_count, -1),
        normalized(raw_qkv_one),
        normalized(raw_proj_one),
        normalized(raw_merge),
        normalized(raw_qkv_two),
        normalized(raw_proj_two),
    )


def solution(mesh):
    in_specs = (
        P(None, "lat", "lon"),
        P(None, "lat", "lon"),
        P(None, "lat"),
        P(None, "lat"),
        P(),
        P(),
        P(),
        P(),
        P(),
        P(),
        P(),
        P(),
        P(),
        P(),
    )
    out_specs = (P(None, "lat", "lon"), P(None, "lat", "lon"), P(), P(), P(), P(), P())
    return jax.shard_map(shards, mesh=mesh, in_specs=in_specs, out_specs=out_specs, check_vma=False)
```

profile of v0, /device:TPU:1, one launch (start us, length us, event | category | flops | bytes accessed | tf_op | source)
XLA Modules:
  0.0 643.8 jit_solution(7995490828892708729)
XLA Ops:
  10.4 4.5 collective-permute-start
  22.6 4.5 copy.138
  27.0 55.6 %gather_fusion.1 = f32[20736,2,6]{2,1,0:T(2,128)} fusion(f32[2,6,3312]{1,0,2:T(2,128)S(1)} %copy.138, s32[21504]{0:T(1024)S(1)} %pad_clamp_fusion), kind=kCustom, calls=%fused_computation.1 | custom fusion | bytes 2073600 | tf_op jit(solution)/shard_map/jvp(jit(_take))/gather | solution.py:122
  82.6 31.0 %copy.139 = f32[144,144,2,6]{0,1,3,2:T(8,128)} copy(f32[144,144,2,6]{3,2,1,0:T(2,128)} %bitcast.176) | data formatting | bytes 1990656 | tf_op jit(solution)/shard_map/jvp(jit(_take))/gather | solution.py:122
  114.2 38.8 %gather_fusion.2 = f32[20736,12]{1,0:T(8,128)} fusion(f32[12,3312]{0,1:T(8,128)S(1)} %bitcast.170, s32[21504]{0:T(1024)S(1)} %pad_clamp_fusion), kind=kCustom, calls=%fused_computation.2 | custom fusion | bytes 2073600 | tf_op jit(solution)/shard_map/jvp(jit(_take))/gather | solution.py:122
  153.0 12.2 %copy.152 = f32[144,144,12]{0,1,2:T(8,128)} copy(f32[144,144,12]{2,1,0:T(8,128)} %bitcast.177) | data formatting | bytes 1990656 | tf_op jit(solution)/shard_map/jvp(jit(_take))/gather | solution.py:122
  168.8 7.4 %collective-permute-start.7 = (bf16[2,6,6,384]{3,2,1,0:T(8,128)(2,1)}, bf16[2,6,6,384]{3,2,1,0:T(8,128)(2,1)}, u32[]{:S(2)}, u32[]{:S(2)}) collective-permute-start(bf16[2,6,6,384]{3,2,1,0:T(8,128)(2,1)} %get-tuple-element.57), channel_id=1, source_target_pairs={{8,0},{16,8},{24,16},{32,24},{40,32},{48,40},{56,48},{64,56},{72,6... | collective-permute-start | bytes 165896 | tf_op jit(solution)/shard_map/ppermute | solution.py:28
  179.8 3.9 reshape.727
  183.8 2.7 copy.134
  186.5 2.6 fusion.95
  193.0 2.9 fusion.5
  196.9 3.5 convert_reduce_fusion
  200.4 3.0 copy.192
  203.5 2.7 fusion.23
  206.2 3.1 copy.141
  209.2 2.5 copy.142
  211.7 2.6 reshape.733
  282.2 3.0 fusion.86
  299.8 2.6 convolution_bitcast_fusion
  306.1 3.2 collective-permute-done.9
  312.9 2.4 reshape.747
  315.3 3.1 copy.165
  318.4 3.0 copy.166
  321.5 3.4 fusion.3
  330.2 4.9 copy.171
  335.1 2.5 copy.172
  337.7 2.9 reshape.751
  347.7 2.7 collective-permute-start.4
  350.5 3.1 collective-permute-done.4
  354.4 8.2 %collective-permute-done.5 = bf16[2,6,6,384]{3,2,1,0:T(8,128)(2,1)S(1)} collective-permute-done((bf16[2,6,6,384]{3,2,1,0:T(8,128)(2,1)S(1)}, bf16[2,6,6,384]{3,2,1,0:T(8,128)(2,1)S(1)}, u32[]{:S(2)}, u32[]{:S(2)}) %collective-permute-start.5) | collective-permute-done | bytes 55328 | tf_op jit(solution)/shard_map/ppermute | solution.py:28
  363.8 6.8 %collective-permute-done.11 = bf16[2,12,6,192]{3,2,1,0:T(8,128)(2,1)S(1)} collective-permute-done((bf16[2,12,6,192]{3,2,1,0:T(8,128)(2,1)S(1)}, bf16[2,12,6,192]{3,2,1,0:T(8,128)(2,1)S(1)}, u32[]{:S(2)}, u32[]{:S(2)}) %collective-permute-start.11) | collective-permute-done | bytes 55328 | tf_op jit(solution)/shard_map/ppermute | solution.py:28
  372.1 247.3 %all-reduce.9.cloned.1.call-done = (f32[192,576]{1,0:T(8,128)}, f32[192,192]{1,0:T(8,128)}, f32[768,384]{1,0:T(8,128)}, f32[384,1152]{1,0:T(8,128)}, f32[384,384]{1,0:T(8,128)}) async-done(((f32[192,576]{1,0:T(8,128)}, f32[192,192]{1,0:T(8,128)}, f32[768,384]{1,0:T(8,128)}, f32[384,1152]{1,0:T(8,128)}, f32[384,384]{1,0:T(8,128)}), (f32[192,576]{1,0:T(8,128)}, f32[192,192]{1,0:T(8,128)}, ...) | async-done | bytes 4128784 | tf_op jit(solution)/shard_map/psum | solution.py:297
  (347 shorter events, 141.4 us)
Async XLA Ops:
  7.2 12.1 %copy-start = (f32[8,12,3312]{2,0,1:T(8,128)S(1)}, f32[8,12,3312]{2,0,1:T(8,128)}, u32[]{:S(2)}) copy-start(f32[8,12,3312]{2,0,1:T(8,128)} %param.21) | copy-start | bytes 3815428
  7.2 9.4 %copy-start.64 = (s32[20736]{0:T(1024)S(1)}, s32[20736]{0:T(1024)}, u32[]{:S(2)}) copy-start(s32[20736]{0:T(1024)} %constant.166) | copy-start | bytes 248836
  7.2 7.7 %copy-start.55 = (bf16[2,6,4608]{2,0,1:T(2,128)(2,1)S(1)}, bf16[2,6,4608]{2,0,1:T(2,128)(2,1)}, u32[]{:S(2)}) copy-start(bf16[2,6,4608]{2,0,1:T(2,128)(2,1)} %param.17) | copy-start | bytes 331780
  7.2 9.3 %copy-start.81 = (s32[1,2]{1,0:T(1,128)S(1)}, s32[1,2]{1,0:T(1,128)}, u32[]{:S(2)}) copy-start(s32[1,2]{1,0:T(1,128)} %param.18) | copy-start | bytes 28
  7.2 612.2 %all-reduce.9.cloned.1.call-start = ((), (), s32[]{:S(2)}) async-start(), calls=%async_computation | async-start | bytes 8454144 | tf_op jit(solution)/shard_map/psum | solution.py:297
  9.6 11.2 %copy-start.18 = (f32[8,6,3312]{2,0,1:T(8,128)S(1)}, f32[8,6,3312]{2,0,1:T(8,128)}, u32[]{:S(2)}) copy-start(f32[8,6,3312]{2,0,1:T(8,128)} %param.20) | copy-start | bytes 1907716
  10.4 155.4 %collective-permute-start = (bf16[2,3,24,192]{3,2,1,0:T(8,128)(2,1)}, bf16[2,3,24,192]{3,2,1,0:T(8,128)(2,1)S(1)}, u32[]{:S(2)}, u32[]{:S(2)}) collective-permute-start(bf16[2,3,24,192]{3,2,1,0:T(8,128)(2,1)} %slice.192), channel_id=1, source_target_pairs={{1,0},{2,1},{3,2},{4,3},{5,4},{6,5},{7,6},{0,7},{9,8},{10,9},{11,1... | collective-permute-start | bytes 165896 | tf_op jit(solution)/shard_map/ppermute | solution.py:28
  16.3 150.9 %collective-permute-start.6 = (bf16[2,3,12,384]{3,2,1,0:T(8,128)(2,1)}, bf16[2,3,12,384]{3,2,1,0:T(8,128)(2,1)}, u32[]{:S(2)}, u32[]{:S(2)}) collective-permute-start(bf16[2,3,12,384]{3,2,1,0:T(8,128)(2,1)} %get-tuple-element.59), channel_id=1, source_target_pairs={{1,0},{2,1},{3,2},{4,3},{5,4},{6,5},{7,6},{0,7},{9,8},{10,9},{11,1... | collective-permute-start | bytes 165896 | tf_op jit(solution)/shard_map/ppermute | solution.py:28
  82.6 31.0 %copy-start.49 = (f32[1,12,3312]{2,0,1:T(1,128)S(1)}, f32[1,12,3312]{2,0,1:T(1,128)}, u32[]{:S(2)}) copy-start(f32[1,12,3312]{2,0,1:T(1,128)} %constant_dynamic-slice_fusion) | copy-start | bytes 476932
  153.0 12.2 %copy-start.69 = (f32[768]{0:T(1024)S(1)}, f32[768]{0:T(1024)}, u32[]{:S(2)}) copy-start(f32[768]{0:T(1024)} %param.23) | copy-start | bytes 9220
  153.0 12.8 %copy-start.29 = (bf16[2,9,24,192]{3,2,1,0:T(8,128)(2,1)S(1)}, bf16[2,9,24,192]{3,2,1,0:T(8,128)(2,1)}, u32[]{:S(2)}) copy-start(bf16[2,9,24,192]{3,2,1,0:T(8,128)(2,1)} %slice.191) | copy-start | bytes 497668
  153.0 14.2 %copy-start.59 = (bf16[2,3,12,384]{3,2,1,0:T(8,128)(2,1)S(1)}, bf16[2,3,12,384]{3,2,1,0:T(8,128)(2,1)}, u32[]{:S(2)}) copy-start(bf16[2,3,12,384]{3,2,1,0:T(8,128)(2,1)} %get-tuple-element.58) | copy-start | bytes 165892
  165.9 10.3 %collective-permute-start.1 = (bf16[2,12,6,192]{3,2,1,0:T(8,128)(2,1)S(1)}, bf16[2,12,6,192]{3,2,1,0:T(8,128)(2,1)S(1)}, u32[]{:S(2)}, u32[]{:S(2)}) collective-permute-start(bf16[2,12,6,192]{3,2,1,0:T(8,128)(2,1)S(1)} %pad_maximum_fusion.9), channel_id=1, source_target_pairs={{8,0},{16,8},{24,16},{32,24},{40,32},{48,40},{56,48},{64,56},{72,6... | collective-permute-start | bytes 165896 | tf_op jit(solution)/shard_map/ppermute | solution.py:28
  168.8 9.7 %copy-start.46 = (bf16[192,576]{1,0:T(8,128)(2,1)S(1)}, bf16[192,576]{1,0:T(8,128)(2,1)}, u32[]{:S(2)}) copy-start(bf16[192,576]{1,0:T(8,128)(2,1)} %param.25) | copy-start | bytes 663556
  168.8 9.7 %copy-start.75 = (f32[192]{0:T(256)S(1)}, f32[192]{0:T(256)}, u32[]{:S(2)}) copy-start(f32[192]{0:T(256)} %param.22) | copy-start | bytes 2308
  168.8 51.9 %collective-permute-start.7 = (bf16[2,6,6,384]{3,2,1,0:T(8,128)(2,1)}, bf16[2,6,6,384]{3,2,1,0:T(8,128)(2,1)}, u32[]{:S(2)}, u32[]{:S(2)}) collective-permute-start(bf16[2,6,6,384]{3,2,1,0:T(8,128)(2,1)} %get-tuple-element.57), channel_id=1, source_target_pairs={{8,0},{16,8},{24,16},{32,24},{40,32},{48,40},{56,48},{64,56},{72,6... | collective-permute-start | bytes 165896 | tf_op jit(solution)/shard_map/ppermute | solution.py:28
  196.9 3.5 copy-start.52
  219.8 10.7 %collective-permute-start.2 = (bf16[2,3,24,192]{3,2,1,0:T(8,128)(2,1)}, bf16[2,3,24,192]{3,2,1,0:T(8,128)(2,1)}, u32[]{:S(2)}, u32[]{:S(2)}) collective-permute-start(bf16[2,3,24,192]{3,2,1,0:T(8,128)(2,1)} %slice.199), channel_id=1, source_target_pairs={{1,0},{2,1},{3,2},{4,3},{5,4},{6,5},{7,6},{0,7},{9,8},{10,9},{11,1... | collective-permute-start | bytes 165896 | tf_op jit(solution)/shard_map/ppermute | solution.py:28
  231.4 4.1 collective-permute-start.3
  295.7 8.0 %collective-permute-start.8 = (bf16[2,3,24,192]{3,2,1,0:T(8,128)(2,1)}, bf16[2,3,24,192]{3,2,1,0:T(8,128)(2,1)}, u32[]{:S(2)}, u32[]{:S(2)}) collective-permute-start(bf16[2,3,24,192]{3,2,1,0:T(8,128)(2,1)} %copy.195), channel_id=1, source_target_pairs={{7,0},{0,1},{1,2},{2,3},{3,4},{4,5},{5,6},{6,7},{15,8},{8,9},{9,10... | collective-permute-start | bytes 165896 | tf_op jit(solution)/shard_map/ppermute | solution.py:28
  299.8 3.8 copy-start.44
  302.4 7.8 %copy-start.58 = (bf16[192,192]{1,0:T(8,128)(2,1)S(1)}, bf16[192,192]{1,0:T(8,128)(2,1)}, u32[]{:S(2)}) copy-start(bf16[192,192]{1,0:T(8,128)(2,1)} %param.26) | copy-start | bytes 221188
  303.6 5.8 copy-start.32
  304.7 4.6 copy-start.30
  304.8 4.5 collective-permute-start.9
  347.7 5.8 collective-permute-start.4
  353.6 9.0 %collective-permute-start.5 = (bf16[2,6,6,384]{3,2,1,0:T(8,128)(2,1)S(1)}, bf16[2,6,6,384]{3,2,1,0:T(8,128)(2,1)S(1)}, u32[]{:S(2)}, u32[]{:S(2)}) collective-permute-start(bf16[2,6,6,384]{3,2,1,0:T(8,128)(2,1)S(1)} %fusion.69), channel_id=1, source_target_pairs={{248,0},{0,8},{8,16},{16,24},{24,32},{32,40},{40,48},{48,56},{56,6... | collective-permute-start | bytes 165896 | tf_op jit(solution)/shard_map/ppermute | solution.py:28
  354.4 8.3 %collective-permute-start.10 = (bf16[2,3,24,192]{3,2,1,0:T(8,128)(2,1)S(1)}, bf16[2,3,24,192]{3,2,1,0:T(8,128)(2,1)S(1)}, u32[]{:S(2)}, u32[]{:S(2)}) collective-permute-start(bf16[2,3,24,192]{3,2,1,0:T(8,128)(2,1)S(1)} %slice.219), channel_id=1, source_target_pairs={{7,0},{0,1},{1,2},{2,3},{3,4},{4,5},{5,6},{6,7},{15,8},{8,9},{9,10... | collective-permute-start | bytes 165896 | tf_op jit(solution)/shard_map/ppermute | solution.py:28
  362.8 7.9 %collective-permute-start.11 = (bf16[2,12,6,192]{3,2,1,0:T(8,128)(2,1)S(1)}, bf16[2,12,6,192]{3,2,1,0:T(8,128)(2,1)S(1)}, u32[]{:S(2)}, u32[]{:S(2)}) collective-permute-start(bf16[2,12,6,192]{3,2,1,0:T(8,128)(2,1)S(1)} %pad_maximum_fusion.7), channel_id=1, source_target_pairs={{248,0},{0,8},{8,16},{16,24},{24,32},{32,40},{40,48},{48,56},{56,6... | collective-permute-start | bytes 165896 | tf_op jit(solution)/shard_map/ppermute | solution.py:28
  619.4 8.3 %copy-start.17 = (f32[768,384]{1,0:T(8,128)S(1)}, f32[768,384]{1,0:T(8,128)}, u32[]{:S(2)}) copy-start(f32[768,384]{1,0:T(8,128)} %get-tuple-element.31) | copy-start | bytes 3538948
  623.7 6.5 %copy-start.14 = (f32[384,1152]{1,0:T(8,128)S(1)}, f32[384,1152]{1,0:T(8,128)}, u32[]{:S(2)}) copy-start(f32[384,1152]{1,0:T(8,128)} %get-tuple-element.32) | copy-start | bytes 5308420
  631.9 4.8 copy-start.1
  (63 other events, 103.3 us)
Sparse Core Ops, SparseCore 0:
  346.4 272.9 all-reduce.8
where the time goes:
time: 656 us; the launch traced here: 644 us
  waiting for transfers between devices  270 us (41%)
  local copies, waits for them, and re-layouts  246 us (38%)
  other arithmetic  46.4 us (7%)
  matrix products  40.4 us (6%)
  starting transfers between devices  20.9 us (3%)
  between operations  19.7 us (3%)
    psum x1, waiting for transfers between devices, shards(): lax.psum((raw_qkv_one, raw_proj_one, raw_merge, raw_qkv_two, raw_proj_two...  247 us
    gather x4, local copies, waits for them, and re-layouts, attend(): full_bias = jnp.take(chosen, relative_table(), axis=3)  138 us
    ppermute x12, waiting for transfers between devices, shifted_2(): return lax.ppermute(block, axis, route)  22.8 us
    ppermute x12, starting transfers between devices, shifted_2(): return lax.ppermute(block, axis, route)  20.9 us
    unnamed x171, local copies, waits for them, and re-layouts  18.2 us
  transfers between devices with their start and end apart: 13, of which 6 were waited for; matrix products, arithmetic and copies ran while one was open for 33% of the time, Pallas kernels for 0%

commit v1 on v0

v1 whole, which is shorter than its diff:
```python
import functools

import jax
import jax.numpy as jnp
import numpy as np
from jax import lax
from jax.experimental import pallas as pl
from jax.experimental.pallas import tpu as pltpu
from jax.sharding import PartitionSpec as P

MESH = pl.DeviceIdType.MESH
BF = jnp.bfloat16
F32 = jnp.float32

C1 = 192
C2 = 384
HEADS1 = 6
HEADS2 = 12
HEAD = 32
ROWS1, COLS1 = 12, 24
ROWS2, COLS2 = 6, 12
HALF_LAT, HALF_LON = 3, 6
BLOCK = 80
VALID = 72
SPAN = 138

norm_epsilon = 1e-05
grad_epsilon = 1e-06
masked_score = -1e30
score_scale = HEAD**-0.5

VM = pl.BlockSpec(memory_space=pltpu.VMEM)
SM = pl.BlockSpec(memory_space=pltpu.SMEM)


def params(**more):
    return pltpu.CompilerParams(vmem_limit_bytes=60 * 1024 * 1024, **more)


def zone_starts(rows, cols):
    sizes = [
        2 * (rows - HALF_LAT) * (cols - HALF_LON),
        2 * HALF_LAT * (cols - HALF_LON),
        2 * (rows - HALF_LAT) * HALF_LON,
        2 * HALF_LAT * HALF_LON,
    ]
    padded = [-(-size // 16) * 16 for size in sizes]
    starts = [sum(padded[:i]) for i in range(4)]
    return starts, padded


def group_index(rows, cols, z, r, c, moved):
    starts, _ = zone_starts(rows, cols)
    if moved:
        far_r, far_c = r >= rows - HALF_LAT, c >= cols - HALF_LON
        r_in = r - (rows - HALF_LAT) if far_r else r
        c_in = c - (cols - HALF_LON) if far_c else c
    else:
        far_r, far_c = r < HALF_LAT, c < HALF_LON
        r_in = r if far_r else r - HALF_LAT
        c_in = c if far_c else c - HALF_LON
    width = HALF_LON if far_c else cols - HALF_LON
    return starts[int(far_r) + 2 * int(far_c)] + (r_in * width + c_in) * 2 + z


def window_index(z, r, c):
    return (((r // 6) * 2 + c // 12) * 2 + z) * BLOCK + (r % 6) * 12 + c % 12


def merge_index(z, r, c):
    part = (r % 2) * 2 + c % 2
    return part * 2 * BLOCK + z * BLOCK + (r // 2) * 12 + c // 2


def order_rows():
    maps = np.full((16, 768), -1, np.int32)
    gi = functools.partial(group_index, ROWS1, COLS1)
    gj = functools.partial(group_index, ROWS2, COLS2)
    for z in range(2):
        for r in range(ROWS1):
            for c in range(COLS1):
                t = (c * 2 + z) * 16 + r
                t_other = (c * 2 + 1 - z) * 16 + r
                win = window_index(z, r, c)
                mer = merge_index(z, r, c)
                maps[0, t] = gi(z, r, c, False)
                maps[2, gi(z, r, c, True)] = window_index(1 - z, r, c)
                maps[3, win] = gi(z, r, c, False)
                maps[4, gi(z, r, c, True)] = mer
                maps[5, mer] = gi(z, r, c, True)
                maps[8, gi(z, r, c, False)] = win
                maps[9, win] = gi(z, r, c, True)
                maps[10, gi(z, r, c, False)] = t_other
        for r in range(ROWS2):
            for c in range(COLS2):
                t = (c * 2 + z) * 8 + r
                t_other = (c * 2 + 1 - z) * 8 + r
                n = z * BLOCK + r * 12 + c
                maps[1, t] = gj(z, r, c, False)
                maps[6, gj(z, r, c, True)] = (1 - z) * BLOCK + r * 12 + c
                maps[7, n] = gj(z, r, c, True)
                maps[11, gj(z, r, c, False)] = t_other
    return maps


MAPS = order_rows()
STARTS1, PADDED1 = zone_starts(ROWS1, COLS1)
STARTS2, PADDED2 = zone_starts(ROWS2, COLS2)
GROUP1 = sum(PADDED1)
GROUP2 = sum(PADDED2)
HALO1 = GROUP1 - PADDED1[0]
HALO2 = GROUP2 - PADDED2[0]
WIN1 = 8 * BLOCK
WIN2 = 2 * BLOCK


def reorder(maps_ref, which, rows, source):
    width = source.shape[0]
    target = maps_ref[which : which + 1, :width]
    chosen = lax.broadcasted_iota(jnp.int32, (rows, width), 0) == target
    one_hot = jnp.where(chosen, 1.0, 0.0).astype(BF)
    return jnp.dot(one_hot, source, preferred_element_type=F32)


def dot_t(a, b):
    return lax.dot_general(a, b, (((1,), (1,)), ((), ())), preferred_element_type=F32)


def t_dot(a, b):
    return lax.dot_general(a, b, (((0,), (0,)), ((), ())), preferred_element_type=F32)


def dot(a, b):
    return jnp.dot(a, b, preferred_element_type=F32)


def standard(x):
    centre = jnp.mean(x, axis=-1, keepdims=True)
    spread = x - centre
    second = jnp.mean(spread * spread, axis=-1, keepdims=True)
    rstd = lax.rsqrt(second + norm_epsilon)
    return spread * rstd, rstd


def head_stack(value, heads):
    lane_head = lax.broadcasted_iota(jnp.int32, value.shape, 1) // HEAD
    zero = jnp.zeros_like(value)
    return jnp.concatenate([jnp.where(lane_head == h, value, zero) for h in range(heads)], axis=0)


def head_join(stacked, heads):
    rows = stacked.shape[0] // heads
    lane_head = lax.broadcasted_iota(jnp.int32, (rows, stacked.shape[1]), 1) // HEAD
    total = jnp.zeros((rows, stacked.shape[1]), F32)
    for h in range(heads):
        total = jnp.where(lane_head == h, stacked[h * rows : (h + 1) * rows], total)
    return total


def attention_fwd(q, k, v, bias, heads):
    scores = dot_t(head_stack(q, heads), k) * score_scale + bias[:, :BLOCK]
    top = jnp.max(scores, axis=-1, keepdims=True)
    weights = jnp.exp(scores - top)
    probs = (weights / jnp.sum(weights, axis=-1, keepdims=True)).astype(BF)
    return probs, head_join(dot(probs, v), heads).astype(BF)


def attention_bwd(q, k, v, probs, d_att, heads):
    d_stack = head_stack(d_att, heads)
    d_probs = dot_t(d_stack, v)
    p = probs.astype(F32)
    weighted = p * d_probs
    d_scores = (weighted - p * jnp.sum(weighted, axis=-1, keepdims=True)).astype(BF)
    d_q = head_join(dot(d_scores, k), heads) * score_scale
    d_k = t_dot(d_scores, head_stack(q, heads)) * score_scale
    d_v = t_dot(probs, d_stack)
    return d_q.astype(BF), d_k.astype(BF), d_v.astype(BF)


def norm_bwd(dy_parts, hats, rstd, width):
    first = sum(jnp.sum(dy, axis=-1, keepdims=True) for dy in dy_parts) / width
    second = sum(jnp.sum(dy * hat, axis=-1, keepdims=True) for dy, hat in zip(dy_parts, hats)) / width
    return [rstd * (dy - first - hat * second) for dy, hat in zip(dy_parts, hats)]


def pack_kernel(maps_ref, tokens_ref, cot_ref, group_ref, cot_group_ref, rows_ref, cot_rows_ref):
    rows_ref[...] = jnp.zeros_like(rows_ref)
    cot_rows_ref[...] = jnp.zeros_like(cot_rows_ref)
    for z in range(2):
        level = tokens_ref[z].astype(F32)
        cot = cot_ref[z].astype(F32)
        for c in range(COLS1):
            start = (c * 2 + z) * 16
            rows_ref[start : start + ROWS1, :] = level[:, c * C1 : (c + 1) * C1]
        for c in range(COLS2):
            start = (c * 2 + z) * 8
            cot_rows_ref[start : start + ROWS2, :] = cot[:, c * C2 : (c + 1) * C2]
    group_ref[...] = reorder(maps_ref, 0, GROUP1, rows_ref[...].astype(BF)).astype(BF)
    cot_group_ref[...] = reorder(maps_ref, 1, GROUP2, cot_rows_ref[...].astype(BF)).astype(BF)


def bias_kernel(kinds1_ref, kinds2_ref, table1_ref, table2_ref, spread_ref, bias1_ref, bias2_ref, seg_ref, wide_ref):
    is_last = lax.axis_index("lat") == lax.axis_size("lat") - 1
    seg_ref[...] = jnp.zeros_like(seg_ref)
    jobs = [(table1_ref[kinds1_ref[0, band]], HEADS1, band == 1) for band in range(2)]
    jobs.append((table2_ref[kinds2_ref[0, 0]], HEADS2, True))
    base = 0
    plans = []
    for number, (table, heads, last_band) in enumerate(jobs):
        for z in range(2):
            for a in range(6):
                start = z * 2484 + a * SPAN
                seg_ref.at[0][pl.ds(base + a, heads, stride=8), :] = table[:, start : start + 128]
                seg_ref.at[1][pl.ds(base + a, heads, stride=8), :] = table[:, start + SPAN - 128 : start + SPAN]
            for h in range(heads):
                plans.append((number, z, h, last_band, base + h * 8))
            base += heads * 8
    segs = jnp.concatenate([seg_ref[0], seg_ref[1]], axis=1)
    high = segs.astype(BF)
    rest = segs - high.astype(F32)
    middle = rest.astype(BF)
    low = (rest - middle.astype(F32)).astype(BF)
    for b in range(12):
        spread = spread_ref[:, b * 128 : (b + 1) * 128]
        wide_ref[:, b * 128 : (b + 1) * 128] = dot(high, spread) + dot(middle, spread) + dot(low, spread)
    bias1_ref[...] = jnp.zeros_like(bias1_ref)
    bias2_ref[...] = jnp.zeros_like(bias2_ref)
    for number, z, h, last_band, row in plans:
        for b in range(12):
            piece = wide_ref[row : row + 6, b * 128 : (b + 1) * 128]
            if number < 2:
                bias1_ref.at[number * 2 + z][pl.ds(h * BLOCK + b, 6, stride=12), :] = piece
            else:
                bias2_ref.at[z][pl.ds(h * BLOCK + b, 6, stride=12), :] = piece
    for ref, which, heads in ((bias1_ref, (2, 3), HEADS1), (bias1_ref, (0, 1), HEADS1), (bias2_ref, (0, 1), HEADS2)):
        rows = heads * BLOCK
        key = lax.broadcasted_iota(jnp.int32, (rows, 128), 1)
        row = lax.broadcasted_iota(jnp.int32, (rows, 128), 0) % BLOCK
        blocked = key >= VALID
        if not (ref is bias1_ref and which == (0, 1)):
            blocked = blocked | (((key < 36) != (row < 36)) & is_last)
        for i in which:
            ref[i] = jnp.where(blocked, masked_score, ref[i])


def first_kernel(
    maps_ref, group_ref, halo_ref, bias_ref, gain_ref, qkv_ref, proj_ref,
    out_ref, x_ref, normed_ref, q_ref, k_ref, v_ref, probs_ref, att_ref,
):
    source = jnp.concatenate([group_ref[: PADDED1[0]], halo_ref[...]], axis=0)
    x = reorder(maps_ref, 2, WIN1, source)
    x_ref[...] = x.astype(BF)
    hat, _ = standard(x)
    normed = (hat * gain_ref[...]).astype(BF)
    normed_ref[...] = normed
    packed = dot(normed, qkv_ref[...]).astype(BF)
    q_ref[...] = packed[:, :C1]
    k_ref[...] = packed[:, C1 : 2 * C1]
    v_ref[...] = packed[:, 2 * C1 :]

    @pl.loop(0, 8)
    def _(block):
        here = pl.ds(pl.multiple_of(block * BLOCK, 16), BLOCK)
        bias = bias_ref[(block // 4) * 2 + block % 2]
        probs, att = attention_fwd(q_ref[here, :], k_ref[here, :], v_ref[here, :], bias, HEADS1)
        probs_ref[pl.ds(pl.multiple_of(block * BLOCK * HEADS1, 16), BLOCK * HEADS1), :] = probs
        att_ref[here, :] = att

    block_one = (x_ref[...].astype(F32) + dot(att_ref[...], proj_ref[...])).astype(BF)
    out_ref[...] = reorder(maps_ref, 3, GROUP1, block_one).astype(BF)


def put_tiles(ref, start, value):
    rows = value.shape[0]
    for j in range(value.shape[1] // 128):
        ref[start + j * rows : start + (j + 1) * rows, :] = value[:, j * 128 : (j + 1) * 128].astype(BF)


MERGE_AT = 0
QKV2_AT = 3 * 4 * C1
PROJ2_AT = QKV2_AT + 9 * C2
ONE_AT = PROJ2_AT + 3 * C2
SUM_ROWS = 8192
TOP_ROWS = ONE_AT


def middle_kernel(
    maps_ref, group_ref, halo_ref, cot_ref, cot_halo_ref, bias_ref, gain_merge_ref, gain_ref, merge_ref, qkv_ref,
    proj_ref, d_group_ref, result_ref, sums_ref, nm_ref, raw_ref,
):
    source = jnp.concatenate([group_ref[: PADDED1[0]], halo_ref[...]], axis=0)
    grouped = reorder(maps_ref, 4, 4 * WIN2, source)
    parts = [grouped[i * WIN2 : (i + 1) * WIN2] for i in range(4)]
    width = 4 * C1
    centre = sum(jnp.sum(part, axis=-1, keepdims=True) for part in parts) / width
    spreads = [part - centre for part in parts]
    second = sum(jnp.sum(s * s, axis=-1, keepdims=True) for s in spreads) / width
    rstd_m = lax.rsqrt(second + norm_epsilon)
    hats_m = [s * rstd_m for s in spreads]
    gains_m = [gain_merge_ref[:, i * C1 : (i + 1) * C1] for i in range(4)]
    weights_m = [merge_ref[i * C1 : (i + 1) * C1, :] for i in range(4)]
    merged = jnp.zeros((WIN2, C2), F32)
    for i in range(4):
        nm_ref[i] = (hats_m[i] * gains_m[i]).astype(BF)
        merged = merged + dot(nm_ref[i], weights_m[i])
    x2 = merged.astype(BF).astype(F32)
    hat2, rstd2 = standard(x2)
    normed2 = (hat2 * gain_ref[...]).astype(BF)
    packed2 = dot(normed2, qkv_ref[...]).astype(BF)

    saved = []
    for z in range(2):
        rows = packed2[z * BLOCK : (z + 1) * BLOCK]
        q, k, v = rows[:, :C2], rows[:, C2 : 2 * C2], rows[:, 2 * C2 :]
        probs, att = attention_fwd(q, k, v, bias_ref[z], HEADS2)
        saved.append((q, k, v, probs, att))
    att2 = jnp.concatenate([s[4] for s in saved], axis=0)
    block_two = (x2 + dot(att2, proj_ref[...])).astype(BF)
    result_ref[...] = reorder(maps_ref, 7, GROUP2, block_two).astype(BF)

    cot_source = jnp.concatenate([cot_ref[: PADDED2[0]], cot_halo_ref[...]], axis=0)
    d_out = reorder(maps_ref, 6, WIN2, cot_source).astype(BF)
    raw_ref[:C2, :C2] = t_dot(att2, d_out)
    put_tiles(sums_ref, PROJ2_AT, raw_ref[:C2, :C2])
    d_att = dot_t(d_out, proj_ref[...]).astype(BF)
    pulled = []
    for z in range(2):
        q, k, v, probs, _ = saved[z]
        pulled.append(attention_bwd(q, k, v, probs, d_att[z * BLOCK : (z + 1) * BLOCK], HEADS2))
    d_packed = [jnp.concatenate([pulled[0][i], pulled[1][i]], axis=0) for i in range(3)]
    d_normed = jnp.zeros((WIN2, C2), F32)
    for i in range(3):
        put_tiles(sums_ref, QKV2_AT + 3 * i * C2, t_dot(normed2, d_packed[i]))
        d_normed = d_normed + dot_t(d_packed[i], qkv_ref[:, i * C2 : (i + 1) * C2])
    dy = d_normed.astype(BF).astype(F32) * gain_ref[...]
    d_x2 = d_out.astype(F32) + norm_bwd([dy], [hat2], rstd2, C2)[0]
    d_merged = d_x2.astype(BF)

    dys = []
    for i in range(4):
        raw_ref[i * C1 : (i + 1) * C1, :] = t_dot(nm_ref[i], d_merged)
        dys.append(dot_t(d_merged, weights_m[i]).astype(BF).astype(F32) * gains_m[i])
    put_tiles(sums_ref, MERGE_AT, raw_ref[...])
    d_parts = norm_bwd(dys, hats_m, rstd_m, width)
    d_grouped = jnp.concatenate([d.astype(BF) for d in d_parts], axis=0)
    d_group_ref[...] = reorder(maps_ref, 5, GROUP1, d_grouped).astype(BF)


def last_kernel(
    maps_ref, group_ref, halo_ref, gain_ref, qkv_ref, proj_ref, x_ref, normed_ref, q_ref, k_ref, v_ref, probs_ref,
    att_ref, sums_ref, d_group_ref, all_ref, d_att_ref, dq_ref, dk_ref, dv_ref,
):
    source = jnp.concatenate([group_ref[: PADDED1[0]], halo_ref[...]], axis=0)
    d_out = reorder(maps_ref, 8, WIN1, source).astype(BF)
    d_att_ref[...] = dot_t(d_out, proj_ref[...]).astype(BF)

    @pl.loop(0, 8)
    def _(block):
        here = pl.ds(pl.multiple_of(block * BLOCK, 16), BLOCK)
        probs = probs_ref[pl.ds(pl.multiple_of(block * BLOCK * HEADS1, 16), BLOCK * HEADS1), :]
        d_q, d_k, d_v = attention_bwd(q_ref[here, :], k_ref[here, :], v_ref[here, :], probs, d_att_ref[here, :], HEADS1)
        dq_ref[here, :] = d_q
        dk_ref[here, :] = d_k
        dv_ref[here, :] = d_v

    normed = normed_ref[...]
    d_packed = jnp.concatenate([dq_ref[...], dk_ref[...], dv_ref[...]], axis=1)
    raw_one = jnp.concatenate([t_dot(normed, d_packed), t_dot(att_ref[...], d_out)], axis=1)
    put_tiles(all_ref, ONE_AT, raw_one)
    all_ref[:TOP_ROWS, :] = sums_ref[...]
    all_ref[ONE_AT + 6 * C1 :, :] = jnp.zeros((SUM_ROWS - ONE_AT - 6 * C1, 128), BF)
    d_normed = dot_t(d_packed, qkv_ref[...])
    hat, rstd = standard(x_ref[...].astype(F32))
    dy = d_normed.astype(BF).astype(F32) * gain_ref[...]
    d_x = d_out.astype(F32) + norm_bwd([dy], [hat], rstd, C1)[0]
    d_group_ref[...] = reorder(maps_ref, 9, GROUP1, d_x.astype(BF)).astype(BF)


def final_kernel(
    maps_ref, d_group_ref, d_halo_ref, res_ref, res_halo_ref, sums_ref,
    result_ref, d_tokens_ref, qkv1_ref, proj1_ref, merge_ref, qkv2_ref, proj2_ref,
):
    source = jnp.concatenate([d_group_ref[: PADDED1[0]], d_halo_ref[...]], axis=0)
    rows = reorder(maps_ref, 10, 32 * COLS1, source)
    res_source = jnp.concatenate([res_ref[: PADDED2[0]], res_halo_ref[...]], axis=0)
    res_rows = reorder(maps_ref, 11, 16 * COLS2, res_source)
    for z in range(2):
        pieces = [rows[(c * 2 + z) * 16 : (c * 2 + z) * 16 + 16] for c in range(COLS1)]
        for c in range(0, COLS1, 2):
            pair = jnp.concatenate([pieces[c], pieces[c + 1]], axis=1).astype(BF)
            d_tokens_ref[z, :, c * C1 : (c + 2) * C1] = pair[:ROWS1]
        for c in range(COLS2):
            start = (c * 2 + z) * 8
            result_ref[z, :, c * C2 : (c + 1) * C2] = res_rows[start : start + 8].astype(BF)[:ROWS2]

    def section(start, rows, lanes):
        tiles = [sums_ref[start + j * rows : start + (j + 1) * rows, :].astype(F32) for j in range(lanes // 128)]
        return tiles

    def norm_scale(tiles, count):
        total = sum(jnp.sum(t * t, axis=0, keepdims=True) for t in tiles)
        total = jnp.sum(total, axis=1, keepdims=True)
        return lax.rsqrt(total / count + grad_epsilon)

    for ref, start, shape in ((merge_ref, MERGE_AT, (4 * C1, C2)), (qkv2_ref, QKV2_AT, (C2, 3 * C2)), (proj2_ref, PROJ2_AT, (C2, C2))):
        tiles = section(start, *shape)
        scale = norm_scale(tiles, shape[0] * shape[1])
        for j, tile in enumerate(tiles):
            ref[:, j * 128 : (j + 1) * 128] = (tile * scale).astype(BF)
    tiles = section(ONE_AT, C1, 4 * C1)
    halves = lax.broadcasted_iota(jnp.int32, (C1, 128), 1) < 64
    zero = jnp.zeros((C1, 128), F32)
    qkv_tiles = tiles[:4] + [jnp.where(halves, tiles[4], zero)]
    proj_tiles = [jnp.where(halves, zero, tiles[4]), tiles[5]]
    scale = norm_scale(qkv_tiles, 3 * C1 * C1)
    for j in range(4):
        qkv1_ref[:, j * 128 : (j + 1) * 128] = (tiles[j] * scale).astype(BF)
    qkv1_ref[:, 512:576] = (tiles[4] * scale).astype(BF)[:, :64]
    scale = norm_scale(proj_tiles, C1 * C1)
    both = jnp.concatenate([tiles[4], tiles[5]], axis=1) * scale
    proj1_ref[...] = both[:, 64:].astype(BF)


def neighbour(steps_lat, steps_lon):
    lat, lon = lax.axis_index("lat"), lax.axis_index("lon")
    rows, cols = lax.axis_size("lat"), lax.axis_size("lon")
    return {"lat": lax.rem(lat + rows + steps_lat, rows), "lon": lax.rem(lon + cols + steps_lon, cols)}


ZONE_STEPS = ((1, 0), (0, 1), (1, 1))


def zone_copies(sources, targets, layouts, direction, send_sem, recv_sem):
    copies = []
    for source, target, (starts, padded) in zip(sources, targets, layouts):
        for i, (lat_step, lon_step) in enumerate(ZONE_STEPS):
            number = len(copies)
            copies.append(
                pltpu.make_async_remote_copy(
                    src_ref=source.at[pl.ds(starts[i + 1], padded[i + 1]), :],
                    dst_ref=target.at[pl.ds(starts[i + 1] - padded[0], padded[i + 1]), :],
                    send_sem=send_sem.at[number],
                    recv_sem=recv_sem.at[number],
                    device_id=neighbour(direction * lat_step, direction * lon_step),
                    device_id_type=MESH,
                )
            )
    return copies


LAYOUTS = ((STARTS1, PADDED1), (STARTS2, PADDED2))


def halo_kernel(direction, count, *refs):
    sources, targets, (send_sem, recv_sem) = refs[:count], refs[count : 2 * count], refs[2 * count :]
    barrier = pltpu.get_barrier_semaphore()
    for lat_step, lon_step in ZONE_STEPS:
        pl.semaphore_signal(
            barrier, inc=1, device_id=neighbour(-direction * lat_step, -direction * lon_step), device_id_type=MESH
        )
    pl.semaphore_wait(barrier, 3)
    copies = zone_copies(sources, targets, LAYOUTS, direction, send_sem, recv_sem)
    for copy in copies:
        copy.start()
    for copy in copies:
        copy.wait()


def halo(sources, direction, collective_id):
    count = len(sources)
    shapes = ((HALO1, C1), (HALO2, C2))[:count]
    return pl.pallas_call(
        functools.partial(halo_kernel, direction, count),
        out_shape=tuple(jax.ShapeDtypeStruct(shape, BF) for shape in shapes),
        in_specs=[VM] * count,
        out_specs=(VM,) * count,
        scratch_shapes=[pltpu.SemaphoreType.DMA((3 * count,)), pltpu.SemaphoreType.DMA((3 * count,))],
        compiler_params=params(collective_id=collective_id, has_side_effects=True),
    )(*sources)


def coordinates():
    lat, lon = lax.axis_index("lat"), lax.axis_index("lon")
    depth = lax.axis_size("lon") // 4
    return {
        "x": lax.div(lon, 2 * depth) * 2 + lax.rem(lat, 2),
        "y": lax.div(lat, 2),
        "z": lax.rem(lax.div(lon, 2), depth),
        "core": lax.rem(lon, 2),
    }


def axis_sizes():
    return {"x": 4, "y": lax.axis_size("lat") // 2, "z": lax.axis_size("lon") // 4, "core": 2}


def device_at(place):
    depth = lax.axis_size("lon") // 4
    lon = lax.div(place["x"], 2) * (2 * depth) + place["z"] * 2 + place["core"]
    return {"lat": place["y"] * 2 + lax.rem(place["x"], 2), "lon": lon}


ROUTES = (("x", "y", "z"), ("y", "x", "z"))
PART_ROWS = SUM_ROWS // 2
CORE_ROWS = PART_ROWS // 2


def sum_kernel(
    sums_ref, d_ref, out_ref, d_halo_ref, core_in, core_sum, in_0, in_1, in_2, sum_1, sum_2,
    core_sems, stage_sems, back_sems, back_core_sems, halo_sems,
):
    me, sizes = coordinates(), axis_sizes()

    def partner(axis, step):
        return device_at({**me, axis: lax.rem(me[axis] + sizes[axis] + step, sizes[axis])})

    barrier = pltpu.get_barrier_semaphore()
    greeted = 0
    for axis in ("core", "x", "y", "z"):
        for step in range(1, sizes[axis]):
            pl.semaphore_signal(barrier, inc=1, device_id=partner(axis, step), device_id_type=MESH)
            greeted += 1
    for lat_step, lon_step in ZONE_STEPS:
        pl.semaphore_signal(barrier, inc=1, device_id=neighbour(-lat_step, -lon_step), device_id_type=MESH)
        greeted += 1
    pl.semaphore_wait(barrier, greeted)

    def send(src, dst, sems, number, device):
        copy = pltpu.make_async_remote_copy(
            src_ref=src, dst_ref=dst, send_sem=sems.at[0, number], recv_sem=sems.at[1, number],
            device_id=device, device_id_type=MESH,
        )
        copy.start()
        return copy

    def rows(start, size):
        return pl.ds(pl.multiple_of(start, 16), size)

    pending = []
    counts = [[sizes[axis] for axis in route] for route in ROUTES]
    units = [[CORE_ROWS // n[0], CORE_ROWS // (n[0] * n[1]), CORE_ROWS // (n[0] * n[1] * n[2])] for n in counts]
    spots = [[me[axis] for axis in route] for route in ROUTES]
    other = 1 - me["core"]

    def chunk_of(part, step):
        return lax.rem(spots[part][0] + step, counts[part][0])

    core_copies = {}
    number = 0
    for step in list(range(1, max(counts[0][0], counts[1][0]))) + [0]:
        for part in range(2):
            if step < counts[part][0]:
                size = units[part][0]
                at = chunk_of(part, step) * size
                core_copies[part, step] = send(
                    sums_ref.at[rows(part * PART_ROWS + other * CORE_ROWS + at, size), :],
                    core_in.at[part, rows(at, size), :],
                    core_sems, number, partner("core", 1),
                )
                number += 1
    halo_copies = zone_copies([d_ref], [d_halo_ref], LAYOUTS[:1], 1, halo_sems.at[0], halo_sems.at[1])
    for copy in halo_copies:
        copy.start()

    incoming = (in_0, in_1, in_2)
    numbers = [0]

    def next_number():
        numbers[0] += 1
        return numbers[0] - 1

    stage_copies = {}

    def core_add(part, step):
        core_copies[part, step].wait_recv()
        size = units[part][0]
        at = chunk_of(part, step) * size
        mine = sums_ref[rows(part * PART_ROWS + me["core"] * CORE_ROWS + at, size), :].astype(F32)
        core_sum[part, rows(at, size), :] = (mine + core_in[part, rows(at, size), :].astype(F32)).astype(BF)

    for step in range(1, max(counts[0][0], counts[1][0])):
        for part in range(2):
            if step < counts[part][0]:
                size = units[part][0]
                core_add(part, step)
                stage_copies[part, 0, step] = send(
                    core_sum.at[part, rows(chunk_of(part, step) * size, size), :],
                    in_0.at[part, pl.ds((step - 1) * size, size), :],
                    stage_sems, next_number(), partner(ROUTES[part][0], step),
                )
    for part in range(2):
        core_add(part, 0)

    def add_up(part, stage, own):
        size = units[part][stage]
        total = own.astype(F32)
        for step in range(1, counts[part][stage]):
            stage_copies[part, stage, step].wait_recv()
            total = total + incoming[stage][part, pl.ds((step - 1) * size, size), :].astype(F32)
        return total.astype(BF)

    held = (core_sum, sum_1, sum_2)
    for stage in (1, 2):
        for part in range(2):
            before = units[part][stage - 1]
            if stage == 1:
                own = core_sum[part, rows(spots[part][0] * before, before), :]
            else:
                own = sum_1[part, rows(spots[part][1] * before, before), :]
            held[stage][part, pl.ds(0, before), :] = add_up(part, stage - 1, own)
            size = units[part][stage]
            for step in range(1, counts[part][stage]):
                chunk = lax.rem(spots[part][stage] + step, counts[part][stage])
                stage_copies[part, stage, step] = send(
                    held[stage].at[part, rows(chunk * size, size), :],
                    incoming[stage].at[part, pl.ds((step - 1) * size, size), :],
                    stage_sems, next_number(), partner(ROUTES[part][stage], step),
                )

    def place(part, depth):
        at = part * PART_ROWS + me["core"] * CORE_ROWS
        for stage in range(depth):
            at = at + spots[part][stage] * units[part][stage]
        return at

    back = [0]

    def next_back():
        back[0] += 1
        return back[0] - 1

    back_copies = {}

    def spread_out(part, stage):
        size = units[part][stage]
        mine = out_ref.at[rows(place(part, stage + 1), size), :]
        for step in range(1, counts[part][stage]):
            back_copies[part, stage, step] = send(mine, mine, back_sems, next_back(), partner(ROUTES[part][stage], step))

    def collect(part, stage):
        for step in range(1, counts[part][stage]):
            back_copies[part, stage, step].wait_recv()

    for part in range(2):
        size = units[part][2]
        own = sum_2[part, rows(spots[part][2] * size, size), :]
        out_ref[rows(place(part, 3), size), :] = add_up(part, 2, own)
        spread_out(part, 2)
    for stage in (2, 1):
        for part in range(2):
            collect(part, stage)
            spread_out(part, stage - 1)
    last_copies = []

    def to_core(part, step):
        size = units[part][0]
        spot = lax.rem(spots[part][0] + counts[part][0] - step, counts[part][0])
        piece = out_ref.at[rows(place(part, 0) + spot * size, size), :]
        last_copies.append(send(piece, piece, back_core_sems, len(last_copies), partner("core", 1)))

    for part in range(2):
        to_core(part, 0)
    for step in range(1, max(counts[0][0], counts[1][0])):
        for part in range(2):
            if step < counts[part][0]:
                back_copies[part, 0, step].wait_recv()
                to_core(part, step)
    for copy in last_copies:
        copy.wait()
    for copy in list(core_copies.values()) + list(stage_copies.values()) + list(back_copies.values()):
        copy.wait_send()
    for copy in halo_copies:
        copy.wait()


def sum_all(sums, d_group, collective_id):
    nx, ny, nz = 4, lax.axis_size("lat") // 2, lax.axis_size("lon") // 4
    small = min(nx, ny)
    first = CORE_ROWS - CORE_ROWS // max(nx, ny)
    sum1 = CORE_ROWS // small
    sum2 = CORE_ROWS // (nx * ny)
    firsts = nx + ny
    stage_count = 2 * (nx - 1) + 2 * (ny - 1) + 2 * (nz - 1)
    dma = pltpu.SemaphoreType.DMA
    return pl.pallas_call(
        sum_kernel,
        out_shape=(jax.ShapeDtypeStruct((SUM_ROWS, 128), BF), jax.ShapeDtypeStruct((HALO1, C1), BF)),
        in_specs=[VM, VM],
        out_specs=(VM, VM),
        scratch_shapes=[
            pltpu.VMEM((2, CORE_ROWS, 128), BF),
            pltpu.VMEM((2, CORE_ROWS, 128), BF),
            pltpu.VMEM((2, first, 128), BF),
            pltpu.VMEM((2, sum1, 128), BF),
            pltpu.VMEM((2, sum2, 128), BF),
            pltpu.VMEM((2, sum1, 128), BF),
            pltpu.VMEM((2, sum2, 128), BF),
            dma((2, firsts)),
            dma((2, stage_count)),
            dma((2, stage_count)),
            dma((2, firsts)),
            dma((2, 3)),
        ],
        compiler_params=params(collective_id=collective_id, has_side_effects=True),
    )(sums, d_group)


def spread_matrix():
    wide = np.zeros((256, 12 * 128), np.float32)
    for b in range(12):
        for other in range(6):
            for key in range(12):
                source = other * 23 + b - key + 11
                source = source if source < 128 else source + 256 - SPAN
                wide[source, b * 128 + other * 12 + key] = 1.0
    return wide


def shapes(*entries):
    return tuple(jax.ShapeDtypeStruct(shape, dtype) for shape, dtype in entries)


def local(kernel, out, scratch, *operands, in_specs=None):
    return pl.pallas_call(
        kernel,
        out_shape=shapes(*out),
        in_specs=in_specs or [VM] * len(operands),
        out_specs=(VM,) * len(out),
        scratch_shapes=scratch,
        compiler_params=params(),
    )(*operands)


def shards(
    tokens, cotangent, kinds_one, kinds_two, table_one, table_two, gain_one, gain_merge, gain_two,
    qkv_one, proj_one, merge_weight, qkv_two, proj_two,
):
    maps = jnp.asarray(MAPS)
    spread = jnp.asarray(spread_matrix(), BF)
    gain_one = gain_one.reshape(1, -1)
    gain_merge = gain_merge.reshape(1, -1)
    gain_two = gain_two.reshape(1, -1)

    group, cot_group = local(
        pack_kernel,
        [((GROUP1, C1), BF), ((GROUP2, C2), BF)],
        [pltpu.VMEM((32 * COLS1, C1), F32), pltpu.VMEM((16 * COLS2, C2), F32)],
        maps, tokens, cotangent,
    )
    bias_one, bias_two = local(
        bias_kernel,
        [((4, HEADS1 * BLOCK, 128), F32), ((2, HEADS2 * BLOCK, 128), F32)],
        [pltpu.VMEM((2, 384, 128), F32), pltpu.VMEM((384, 12 * 128), F32)],
        kinds_one, kinds_two, table_one, table_two, spread,
        in_specs=[SM, SM, VM, VM, VM],
    )
    halo_group, halo_cot = halo([group, cot_group], -1, 0)
    act = ((WIN1, C1), BF)
    block_group, x, normed, q, k, v, probs, att = local(
        first_kernel,
        [((GROUP1, C1), BF), act, act, act, act, act, ((8 * HEADS1 * BLOCK, BLOCK), BF), act],
        [],
        maps, group, halo_group, bias_one, gain_one, qkv_one, proj_one,
    )
    (halo_block,) = halo([block_group], -1, 1)
    d_moved, result_group, top_sums = local(
        middle_kernel,
        [((GROUP1, C1), BF), ((GROUP2, C2), BF), ((TOP_ROWS, 128), BF)],
        [pltpu.VMEM((4, WIN2, C1), BF), pltpu.VMEM((4 * C1, C2), F32)],
        maps, block_group, halo_block, cot_group, halo_cot, bias_two, gain_merge, gain_two, merge_weight, qkv_two, proj_two,
    )
    halo_d, halo_result = halo([d_moved, result_group], 1, 2)
    d_group, sums = local(
        last_kernel,
        [((GROUP1, C1), BF), ((SUM_ROWS, 128), BF)],
        [pltpu.VMEM((WIN1, C1), BF) for _ in range(4)],
        maps, d_moved, halo_d, gain_one, qkv_one, proj_one, x, normed, q, k, v, probs, att, top_sums,
    )
    total, halo_tokens = sum_all(sums, d_group, 3)
    return local(
        final_kernel,
        [
            ((2, ROWS2, COLS2 * C2), BF),
            ((2, ROWS1, COLS1 * C1), BF),
            ((C1, 3 * C1), BF),
            ((C1, C1), BF),
            ((4 * C1, C2), BF),
            ((C2, 3 * C2), BF),
            ((C2, C2), BF),
        ],
        [],
        maps, d_group, halo_tokens, result_group, halo_result, total,
    )


def solution(mesh):
    in_specs = (P(None, "lat", "lon"),) * 2 + (P(None, "lat"),) * 2 + (P(),) * 10
    out_specs = (P(None, "lat", "lon"),) * 2 + (P(),) * 5
    return jax.shard_map(shards, mesh=mesh, in_specs=in_specs, out_specs=out_specs, check_vma=False)
```

time: 656 us -> 142 us (0.22); the launches traced: 644 us -> 141 us
  waiting for transfers between devices: 270 us -> 0 us
  local copies, waits for them, and re-layouts: 246 us -> 13.1 us
  Pallas kernels: 0 us -> 126 us
  other arithmetic: 46.4 us -> 0 us
  matrix products: 40.4 us -> 0 us
  starting transfers between devices: 20.9 us -> 0 us
  between operations: 19.7 us -> 1.43 us
    psum x1 -> x0, waiting for transfers between devices: 247 us -> none  [shards(): lax.psum((raw_qkv_one, raw_proj_one, raw_merge, raw_qkv_two, raw_proj_two...]
    gather x6 -> x0, local copies, waits for them, and re-layouts: 144 us -> none  [the longest x4 138 us: attend(): full_bias = jnp.take(chosen, relative_table(), axis=3)]
    pallas_call x0 -> x10, Pallas kernels: none -> 126 us  [the longest x1 45.3 us: sum_all(): pl.pallas_call(sum_kernel, out_shape=(jax.ShapeDtypeStruct((SUM_ROWS, 128...]
    dot_general x27 -> x0, matrix products: 40.4 us -> none  [the longest x6 9.36 us: attend(): jnp.einsum('abdhqk,abdkhe->abdqhe', attn_weights, value_rows, preferred_e...]
    convert_element_type x14 -> x0, local copies, waits for them, and re-layouts: 23.6 us -> none  [the longest x3 5.84 us: merge_tokens(): grouped.astype(jnp.float32)]
    ppermute x12 -> x0, waiting for transfers between devices: 22.8 us -> none  [shifted_2(): return lax.ppermute(block, axis, route)]
    reduce_sum x19 -> x0, other arithmetic: 21.9 us -> none  [the longest x5 6.27 us: normalized(): scale_back = lax.rsqrt(jnp.mean(gradient * gradient) + grad_epsilon)]
    ppermute x12 -> x0, starting transfers between devices: 20.9 us -> none  [shifted_2(): return lax.ppermute(block, axis, route)]
  transfers between devices with their start and end apart: 13 -> 0, of which waited for: 6 -> 0; matrix products, arithmetic and copies ran while one was open for 33% -> 0% of each run, Pallas kernels for 0% -> 0%
where the time goes in v1:
time: 142 us; the launch traced here: 141 us
  Pallas kernels  126 us (89%)
  local copies, waits for them, and re-layouts  13.1 us (9%)
  between operations  1.43 us (1%)
    pallas_call x1, Pallas kernels, sum_all(): pl.pallas_call(sum_kernel, out_shape=(jax.ShapeDtypeStruct((SUM_ROWS, 128...  45.3 us
    pallas_call x6, Pallas kernels, local(): pl.pallas_call(kernel, out_shape=shapes(*out), in_specs=in_specs or [VM]...  44.4 us
    pallas_call x3, Pallas kernels, halo(): pl.pallas_call(functools.partial(halo_kernel, direction, count), out_shap...  36.8 us
    unnamed x6, local copies, waits for them, and re-layouts  7.08 us
    pallas_call x2, local copies, waits for them, and re-layouts, local(): pl.pallas_call(kernel, out_shape=shapes(*out), in_specs=in_specs or [VM]...  3.51 us

profile of v1, /device:TPU:1, one launch (start us, length us, event | category | flops | bytes accessed | tf_op | source)
XLA Modules:
  0.0 141.0 jit_solution(15545045386371925924)
XLA Ops:
  0.6 0.0 copy-start
  1.4 1.2 reshape.25.gain_ref
  2.6 1.3 reshape.24.gain_merge_ref
  3.9 1.6 %copy.24.cot_ref = bf16[2,6,4608]{2,1,0:T(8,128)(2,1)} copy(bf16[2,6,4608]{2,0,1:T(2,128)(2,1)} %param.17) | data formatting | bytes 221184 | tf_op args[1]
  5.5 1.7 %copy.23.tokens_ref = bf16[2,12,4608]{2,1,0:T(8,128)(2,1)} copy(bf16[2,12,4608]{2,0,1:T(2,128)(2,1)} %param.16) | data formatting | bytes 442368 | tf_op args[0]
  7.2 2.4 %shard_map.207 = (bf16[608,192]{1,0:T(8,128)(2,1)}, bf16[192,384]{1,0:T(8,128)(2,1)}) custom-call(s32[16,768]{1,0:T(8,128)} %constant.4.clone.maps_ref, bf16[2,12,4608]{2,1,0:T(8,128)(2,1)} %copy.23.tokens_ref, bf16[2,6,4608]{2,1,0:T(8,128)(2,1)} %copy.24.cot_ref), custom_call_target="tpu_custom_call" | custom-call | tf_op jit(solution)/shard_map/pallas_call | solution.py:724
  9.6 11.3 %shard_map.208 = (bf16[272,192]{1,0:T(8,128)(2,1)}, bf16[144,384]{1,0:T(8,128)(2,1)}) custom-call(bf16[608,192]{1,0:T(8,128)(2,1)} %get-tuple-element.30.refs_0_.group_ref, bf16[192,384]{1,0:T(8,128)(2,1)} %get-tuple-element.31.refs_1_.cot_ref), custom_call_target="tpu_custom_call" | custom-call | tf_op jit(solution)/shard_map/pallas_call | solution.py:472
  20.9 2.2 %copy.25.table1_ref = f32[8,6,3312]{2,1,0:T(8,128)} copy(f32[8,6,3312]{2,0,1:T(8,128)} %param.20) | data formatting | bytes 1271808 | tf_op args[4]
  23.1 0.0 copy-done
  23.1 1.6 %copy.26.table2_ref = f32[8,12,3312]{2,1,0:T(8,128)} copy(f32[8,12,3312]{2,0,1:T(8,128)S(1)} %copy-done) | data formatting | bytes 2543616 | tf_op args[5]
  24.7 6.0 %shard_map.209 = (f32[4,480,128]{2,1,0:T(8,128)}, f32[2,960,128]{2,1,0:T(8,128)}) custom-call(s32[1,2]{1,0:T(1,128)} %kinds1_ref.1, s32[1,1]{1,0:T(1,128)S(6)} %copy.29.kinds2_ref, f32[8,6,3312]{2,1,0:T(8,128)} %copy.25.table1_ref, f32[8,12,3312]{2,1,0:T(8,128)} %copy.26.table2_ref, bf16[256,1536]{1,0:T(8,128)(2,1)} %constant.5.clone.spread_ref), custom_call_target="tpu_custom_call" | custom-call | tf_op jit(solution)/shard_map/pallas_call | solution.py:724
  30.6 9.5 %shard_map.210 = (bf16[608,192]{1,0:T(8,128)(2,1)}, bf16[640,192]{1,0:T(8,128)(2,1)}, bf16[640,192]{1,0:T(8,128)(2,1)}, bf16[640,192]{1,0:T(8,128)(2,1)}, bf16[6...) custom-call(s32[16,768]{1,0:T(8,128)} %constant.4.clone.maps_ref, ...), custom_call_target="tpu_custom_call" | custom-call | tf_op jit(solution)/shard_map/pallas_call | solution.py:724
  40.1 11.6 %shard_map.211.halo_ref = bf16[272,192]{1,0:T(8,128)(2,1)} custom-call(bf16[608,192]{1,0:T(8,128)(2,1)} %get-tuple-element.34.refs_0_.group_ref), custom_call_target="tpu_custom_call" | custom-call | tf_op jit(solution)/shard_map/pallas_call | solution.py:472
  51.7 10.3 %shard_map.212 = (bf16[608,192]{1,0:T(8,128)(2,1)}, bf16[192,384]{1,0:T(8,128)(2,1)}, bf16[6912,128]{1,0:T(8,128)(2,1)}) custom-call(s32[16,768]{1,0:T(8,128)} %constant.4.clone.maps_ref, bf16[608,192]{1,0:T(8,128)(2,1)} %get-tuple-element.34.refs_0_.group_ref, bf16[272,192]{1,0:T(8,128)(2,1)} %shard_map.211.halo_ref, ...), custom_call_target="tpu_custom_call" | custom-call | tf_op jit(solution)/shard_map/pallas_call | solution.py:724
  62.0 13.9 %shard_map.213 = (bf16[272,192]{1,0:T(8,128)(2,1)}, bf16[144,384]{1,0:T(8,128)(2,1)}) custom-call(bf16[608,192]{1,0:T(8,128)(2,1)} %get-tuple-element.37.refs_0_.group_ref, bf16[192,384]{1,0:T(8,128)(2,1)} %get-tuple-element.38.refs_1_.res_ref), custom_call_target="tpu_custom_call" | custom-call | tf_op jit(solution)/shard_map/pallas_call | solution.py:472
  76.0 11.5 %shard_map.214 = (bf16[608,192]{1,0:T(8,128)(2,1)}, bf16[8192,128]{1,0:T(8,128)(2,1)}) custom-call(s32[16,768]{1,0:T(8,128)} %constant.4.clone.maps_ref, bf16[608,192]{1,0:T(8,128)(2,1)} %get-tuple-element.37.refs_0_.group_ref, bf16[272,192]{1,0:T(8,128)(2,1)} %get-tuple-element.39.halo_ref, f32[1,192]{1,0:T(1,128)} %bitcast.2, bf16[192,576]{1,0:T(8,128)(2,1)} %qkv_ref.5, ...), custom_call_target="tpu_custom_call" | custom-call | tf_op jit(solution)/shard_map/pallas_call | solution.py:724
  87.5 45.3 %shard_map.215 = (bf16[8192,128]{1,0:T(8,128)(2,1)}, bf16[272,192]{1,0:T(8,128)(2,1)}) custom-call(bf16[8192,128]{1,0:T(8,128)(2,1)} %get-tuple-element.49.sums_ref, bf16[608,192]{1,0:T(8,128)(2,1)} %get-tuple-element.48.d_ref.d_group_ref), custom_call_target="tpu_custom_call" | custom-call | tf_op jit(solution)/shard_map/pallas_call | solution.py:685
  132.7 4.7 %shard_map.216 = (bf16[2,6,4608]{2,1,0:T(8,128)(2,1)}, bf16[2,12,4608]{2,1,0:T(8,128)(2,1)}, bf16[192,576]{1,0:T(8,128)(2,1)}, bf16[192,192]{1,0:T(8,128)(2,1)},...) custom-call(s32[16,768]{1,0:T(8,128)} %constant.4.clone.maps_ref, ...), custom_call_target="tpu_custom_call" | custom-call | tf_op jit(solution)/shard_map/pallas_call | solution.py:724
  137.5 1.6 %copy.27 = bf16[2,6,4608]{2,0,1:T(2,128)(2,1)} copy(bf16[2,6,4608]{2,1,0:T(8,128)(2,1)} %get-tuple-element.53) | data formatting | bytes 221184 | tf_op jit(solution)/shard_map/pallas_call | solution.py:724
  139.1 1.9 %copy.28 = bf16[2,12,4608]{2,0,1:T(2,128)(2,1)} copy(bf16[2,12,4608]{2,1,0:T(8,128)(2,1)} %get-tuple-element.54) | data formatting | bytes 442368 | tf_op jit(solution)/shard_map/pallas_call | solution.py:724
Async XLA Ops:
  0.6 22.4 %copy-start = (f32[8,12,3312]{2,0,1:T(8,128)S(1)}, f32[8,12,3312]{2,0,1:T(8,128)}, u32[]{:S(2)}) copy-start(f32[8,12,3312]{2,0,1:T(8,128)} %param.21) | copy-start | bytes 3815428
